TPU v7x, 32 devices: a whole 2x2x4 slice. The times are simulated.
32 devices in a mesh: dp: 8 (over z, x), mp: 4 (over y, core).
Axes of the slice: x: 2, y: 2, z: 4, core: 2. Of those that a mesh axis runs over, the one named last changes fastest.
Arguments:
- media: bfloat16 [64, 256, 1536], P('dp', None, 'mp'), may hold values from -6 to 6
- time_table: bfloat16 [8, 1536], P(None, 'mp'), may hold values from -4 to 4
- doc_images: int32 [16], P('dp'), may hold values from 0 to 8, as said below
- plan: int32 [8, 8], P('dp'), may hold values from -1 to 19, as said below
- latents: bfloat16 [64, 1536], replicated, may hold values from -6 to 6
- queries: bfloat16 [64, 1024], P(None, 'mp'), may hold values from -450 to 450
- key_weight: bfloat16 [1536, 1024], P(None, 'mp'), may hold values from -0.15625 to 0.15625
- value_weight: bfloat16 [1536, 1024], P(None, 'mp'), may hold values from -0.15625 to 0.15625
- out_weight: bfloat16 [1024, 1536], P('mp'), may hold values from -0.1875 to 0.1875
- cotangent: bfloat16 [32, 64, 1536], P('dp', None, 'mp'), may hold values from -6 to 6
Outputs:
- resampled: bfloat16 [32, 64, 1536], P('dp', None, 'mp')
- key_grad: float32 [1536, 1024], P('dp', 'mp')
- value_grad: float32 [1536, 1024], P('dp', 'mp')
Inputs may be any that keep to these rules, and one draw needn't show every extreme that they name: `doc_images`: A device's documents fill its image slots from slot 0 in document order and hold 8 images or fewer together; some document holds exactly 8. `plan`: entry s of device d's row is -1 exactly when slot s holds no image, else k * 4 + w with k from 0 to 4 and d + k a device of dp: the image goes to work slot w of device d + k. Each work slot receives at most one image; a device sends at most one image for each k from 1 to 4; some device sends one for every such k and fills its own 4 work slots.
All inputs are finite; a program needn't handle non-finite values.
Results may differ from a plain program's by a relative error of at most 0.0096.
Values may be sent and summed in bfloat16 or wider, within the bound.
No kernel may reach another device: no remote copies, remote signals or barrier semaphores. Data moves between devices by JAX's collectives and lax.ppermute only.
A program may use at most 64 MiB of HBM per device.

v0:
```python
import jax
import jax.numpy as jnp
from jax import lax
from jax.sharding import PartitionSpec as P

HEAD = 64
norm_epsilon = 1e-05


def from_behind(block, axis, distance):
    devices = range(lax.axis_size(axis))
    route = [(i - distance, i) for i in devices if i - distance in devices]
    return lax.ppermute(block, axis, route)


def layer_norm(rows_in):
    average = jnp.mean(rows_in, axis=-1, keepdims=True)
    centred = rows_in - average
    spread = jnp.mean(centred * centred, axis=-1, keepdims=True)
    return centred * lax.rsqrt(spread + norm_epsilon)


def local(
    media,
    time_table,
    doc_images,
    plan,
    latents,
    queries,
    key_weight,
    value_weight,
    out_weight,
    cotangent,
):
    slot_cap = media.shape[0]
    image_tokens = media.shape[1]
    quarter = media.shape[2]
    work_slots = cotangent.shape[0]
    latent_count = cotangent.shape[1]
    reach_steps = slot_cap - work_slots
    model_width = latents.shape[1]
    inner_dev = queries.shape[1]
    head_count = inner_dev // HEAD
    context_rows = image_tokens + latent_count
    slot_iota = jnp.arange(slot_cap, dtype=jnp.int32)
    doc_ends = jnp.cumsum(doc_images)
    starts = doc_ends - doc_images
    start_of = jnp.max(jnp.where(starts[None, :] <= slot_iota[:, None], starts[None, :], 0), axis=1)
    position = slot_iota - start_of
    position_hot = (position[:, None] == slot_iota[None, :]).astype(jnp.bfloat16)
    time_rows = jnp.dot(position_hot, time_table, preferred_element_type=jnp.float32)
    framed = (media.astype(jnp.float32) + time_rows[:, None, :]).astype(jnp.bfloat16)
    plan_codes = plan[0]
    is_live = plan_codes >= 0
    helper = jnp.where(is_live, plan_codes // work_slots, -1)
    target = jnp.where(is_live, plan_codes % work_slots, -1)
    target_hot = (target[:, None] == jnp.arange(work_slots, dtype=jnp.int32)[None, :]) & is_live[
        :, None
    ]
    local_map = (target_hot & (helper == 0)[:, None]).astype(jnp.bfloat16)
    work_rows = jnp.einsum("sw,std->wtd", local_map, framed, preferred_element_type=jnp.float32)
    alive_slot = jnp.sum(local_map.astype(jnp.float32), axis=0)
    for offset in range(1, reach_steps + 1):
        chosen = (target_hot & (helper == offset)[:, None]).astype(jnp.bfloat16)
        picked = jnp.sum(chosen, axis=1)
        image_block = jnp.einsum(
            "s,std->td", picked, framed, preferred_element_type=jnp.float32
        ).astype(jnp.bfloat16)
        slot_mark = jnp.sum(chosen, axis=0)
        got_block, got_mark = from_behind((image_block, slot_mark), "dp", offset)
        work_rows = (
            work_rows
            + got_mark.astype(jnp.float32)[:, None, None]
            * got_block.astype(jnp.float32)[None, :, :]
        )
        alive_slot = alive_slot + got_mark.astype(jnp.float32)
    work_media = work_rows.astype(jnp.bfloat16)
    values32 = work_media.astype(jnp.float32)
    first_sum = jnp.sum(values32, axis=-1, keepdims=True)
    square_sum = jnp.sum(values32 * values32, axis=-1, keepdims=True)
    first_all, square_all = lax.psum((first_sum, square_sum), "mp")
    average = first_all / model_width
    spread = square_all / model_width - average * average
    normed_part = ((values32 - average) * lax.rsqrt(spread + norm_epsilon)).astype(jnp.bfloat16)
    normed, cot_full = (
        lax.all_gather(normed_part, "mp", axis=2, tiled=True),
        lax.all_gather(cotangent, "mp", axis=2, tiled=True),
    )
    normed_flat = normed.reshape(work_slots * image_tokens, model_width)
    latent_norm = layer_norm(latents.astype(jnp.float32)).astype(jnp.bfloat16)
    media_keys = (
        jnp.dot(normed_flat, key_weight, preferred_element_type=jnp.float32)
        .astype(jnp.bfloat16)
        .reshape(work_slots, image_tokens, inner_dev)
    )
    media_values = (
        jnp.dot(normed_flat, value_weight, preferred_element_type=jnp.float32)
        .astype(jnp.bfloat16)
        .reshape(work_slots, image_tokens, inner_dev)
    )
    latent_keys = jnp.dot(latent_norm, key_weight, preferred_element_type=jnp.float32).astype(
        jnp.bfloat16
    )
    latent_values = jnp.dot(latent_norm, value_weight, preferred_element_type=jnp.float32).astype(
        jnp.bfloat16
    )
    key_rows = jnp.concatenate(
        [media_keys, jnp.broadcast_to(latent_keys[None], (work_slots, latent_count, inner_dev))], 1
    )
    value_rows = jnp.concatenate(
        [
            media_values,
            jnp.broadcast_to(latent_values[None], (work_slots, latent_count, inner_dev)),
        ],
        1,
    )
    key_heads = key_rows.reshape(work_slots, context_rows, head_count, HEAD)
    value_heads = value_rows.reshape(work_slots, context_rows, head_count, HEAD)
    query_heads = queries.reshape(latent_count, head_count, HEAD)
    scores = (
        jnp.einsum("qhe,wkhe->whqk", query_heads, key_heads, preferred_element_type=jnp.float32)
        * 0.125
    )
    attention = jax.nn.softmax(scores, axis=-1)
    attention_b = attention.astype(jnp.bfloat16)
    attended = jnp.einsum(
        "whqk,wkhe->wqhe", attention_b, value_heads, preferred_element_type=jnp.float32
    ).astype(jnp.bfloat16)
    attended_flat = attended.reshape(work_slots * latent_count, inner_dev)
    partial_out = jnp.dot(attended_flat, out_weight, preferred_element_type=jnp.float32).reshape(
        work_slots, latent_count, model_width
    )
    summed_heads = lax.psum_scatter(
        partial_out.astype(jnp.bfloat16), "mp", scatter_dimension=2, tiled=True
    ).astype(jnp.float32)
    latent_part = lax.dynamic_slice_in_dim(
        latents, lax.axis_index("mp") * quarter, quarter, 1
    ).astype(jnp.float32)
    resampled = ((latent_part[None] + summed_heads) * alive_slot[:, None, None]).astype(
        jnp.bfloat16
    )
    cot_live = cot_full * alive_slot.astype(jnp.bfloat16)[:, None, None]
    grad_attended = lax.dot_general(
        cot_live.reshape(work_slots * latent_count, model_width),
        out_weight,
        (((1,), (1,)), ((), ())),
        preferred_element_type=jnp.float32,
    ).astype(jnp.bfloat16)
    grad_heads = grad_attended.reshape(work_slots, latent_count, head_count, HEAD)
    grad_weights = jnp.einsum(
        "wqhe,wkhe->whqk", grad_heads, value_heads, preferred_element_type=jnp.float32
    )
    row_dot = jnp.sum(attention * grad_weights, axis=-1, keepdims=True)
    grad_scores = attention * (grad_weights - row_dot)
    grad_keys = (
        (
            jnp.einsum(
                "whqk,qhe->wkhe",
                grad_scores,
                query_heads.astype(jnp.float32),
                precision=lax.Precision.HIGHEST,
            )
            * 0.125
        )
        .astype(jnp.bfloat16)
        .reshape(work_slots, context_rows, inner_dev)
    )
    grad_values = (
        jnp.einsum("whqk,wqhe->wkhe", attention_b, grad_heads, preferred_element_type=jnp.float32)
        .astype(jnp.bfloat16)
        .reshape(work_slots, context_rows, inner_dev)
    )
    media_grads = jnp.concatenate(
        [grad_keys[:, :image_tokens], grad_values[:, :image_tokens]], 2
    ).reshape(work_slots * image_tokens, 2 * inner_dev)
    latent_grads = jnp.concatenate(
        [
            jnp.sum(grad_keys[:, image_tokens:].astype(jnp.float32), axis=0),
            jnp.sum(grad_values[:, image_tokens:].astype(jnp.float32), axis=0),
        ],
        1,
    )
    latent_norm32 = latent_norm.astype(jnp.float32)
    inverse_slots = 1.0 / (lax.axis_size("dp") * work_slots)
    media_part = lax.dot_general(
        normed_flat, media_grads, (((0,), (0,)), ((), ())), preferred_element_type=jnp.float32
    )
    latent_term = lax.dot_general(
        latent_norm32,
        latent_grads,
        (((0,), (0,)), ((), ())),
        precision=lax.Precision.HIGHEST,
        preferred_element_type=jnp.float32,
    )
    shares = lax.psum_scatter(
        (media_part + latent_term) * inverse_slots, "dp", scatter_dimension=0, tiled=True
    )
    return (resampled, shares[:, :inner_dev], shares[:, inner_dev:])


def solution(mesh):
    return jax.shard_map(
        local,
        mesh=mesh,
        in_specs=(
            P("dp", None, "mp"),
            P(None, "mp"),
            P("dp"),
            P("dp", None),
            P(),
            P(None, "mp"),
            P(None, "mp"),
            P(None, "mp"),
            P("mp", None),
            P("dp", None, "mp"),
        ),
        out_specs=(P("dp", None, "mp"), P("dp", "mp"), P("dp", "mp")),
        check_vma=False,
    )
```

profile of v0, /device:TPU:0, one launch (start us, length us, event | category | flops | bytes accessed | tf_op | source)
XLA Modules:
  0.0 241.2 jit_solution(2323015476926273709)
XLA Ops:
  11.1 1.7 add_convert_fusion
  14.2 4.9 %collective-permute-start.1 = (bf16[256,384]{1,0:T(8,128)(2,1)S(1)}, bf16[256,384]{1,0:T(8,128)(2,1)S(1)}, u32[]{:S(2)}, u32[]{:S(2)}) collective-permute-start(bf16[256,384]{1,0:T(8,128)(2,1)S(1)} %bitcast.118), channel_id=1, source_target_pairs={{0,4},{4,8},{8,12},{12,16},{16,20},{20,24},{24,28},{1,5},{5,9},{9,... | collective-permute-start | bytes 589832 | tf_op jit(solution)/shard_map/ppermute | solution.py:13
  20.2 3.5 %collective-permute-start.3 = (bf16[256,384]{1,0:T(8,128)(2,1)S(1)}, bf16[256,384]{1,0:T(8,128)(2,1)S(1)}, u32[]{:S(2)}, u32[]{:S(2)}) collective-permute-start(bf16[256,384]{1,0:T(8,128)(2,1)S(1)} %bitcast.119), channel_id=1, source_target_pairs={{0,8},{4,12},{8,16},{12,20},{16,24},{20,28},{1,9},{5,13},{9,17},{1... | collective-permute-start | bytes 589832 | tf_op jit(solution)/shard_map/ppermute | solution.py:13
  24.8 4.5 %collective-permute-start.5 = (bf16[256,384]{1,0:T(8,128)(2,1)S(1)}, bf16[256,384]{1,0:T(8,128)(2,1)S(1)}, u32[]{:S(2)}, u32[]{:S(2)}) collective-permute-start(bf16[256,384]{1,0:T(8,128)(2,1)S(1)} %bitcast.120), channel_id=1, source_target_pairs={{0,12},{4,16},{8,20},{12,24},{16,28},{1,13},{5,17},{9,21},{13,25},... | collective-permute-start | bytes 589832 | tf_op jit(solution)/shard_map/ppermute | solution.py:13
  30.4 1.9 collective-permute-start.7
  32.4 2.7 %collective-permute-start = (bf16[4]{0:T(256)(128)(2,1)S(1)}, bf16[4]{0:T(256)(128)(2,1)S(1)}, u32[]{:S(2)}, u32[]{:S(2)}) collective-permute-start(bf16[4]{0:T(256)(128)(2,1)S(1)} %get-tuple-element.5), channel_id=1, source_target_pairs={{0,4},{4,8},{8,12},{12,16},{16,20},{20,24},{24,28},{1,5},{5,9},{9,... | collective-permute-start | bytes 32 | tf_op jit(solution)/shard_map/ppermute | solution.py:13
  36.4 14.4 %collective-permute-start.6 = (bf16[4]{0:T(256)(128)(2,1)S(1)}, bf16[4]{0:T(256)(128)(2,1)S(1)}, u32[]{:S(2)}, u32[]{:S(2)}) collective-permute-start(bf16[4]{0:T(256)(128)(2,1)S(1)} %get-tuple-element.14), channel_id=1, source_target_pairs={{0,16},{4,20},{8,24},{12,28},{1,17},{5,21},{9,25},{13,29},{2,18},{... | collective-permute-start | bytes 32 | tf_op jit(solution)/shard_map/ppermute | solution.py:13
  57.4 3.6 %convert_reduce_fusion = (f32[4,256]{0,1:T(8,128)S(1)}, f32[4,256]{0,1:T(8,128)S(1)}, bf16[4,256,384]{2,0,1:T(4,128)(2,1)S(1)}) fusion(f32[256,384]{1,0:T(8,128)S(1)} %convert_element_type.173, f32[4]{0:T(128)S(1)} %convert_element_type.171, f32[256,384]{1,0:T(8,128)S(1)} %convert_element_type.169, f32[4]{0:T(128)S(1)} %convert_element_type.167, ...), kind=kOutput, calls=%fused_computation.8 | convolution fusion | flops 11401248 | bytes 3940456 | tf_op jit(solution)/shard_map/sw,std->wtd/dot_general | solution.py:61
  61.1 12.9 %all-reduce = (f32[4,256,1]{0,1,2:T(8,128)S(1)}, f32[4,256,1]{0,1,2:T(8,128)S(1)}) all-reduce(f32[4,256,1]{0,1,2:T(8,128)S(1)} %bitcast.123, f32[4,256,1]{0,1,2:T(8,128)S(1)} %bitcast.122), channel_id=1, replica_groups=mesh['dp'=8,'mp'=4] {'mp'}, use_global_device_ids=true, to_apply=%region_13.14 | all-reduce | flops 2048 | bytes 16384 | tf_op jit(solution)/shard_map/psum | solution.py:81
  77.3 9.5 %all_gather.7 = bf16[4,64,1536]{2,1,0:T(8,128)(2,1)S(1)} all-gather(bf16[4,64,384]{2,1,0:T(8,128)(2,1)S(1)} %copy-done.8), channel_id=1, replica_groups=mesh['dp'=8,'mp'=4] {'mp'}, dimensions={2}, use_global_device_ids=true | all-gather | bytes 983040 | tf_op jit(solution)/shard_map/all_gather | solution.py:87
  87.6 25.2 %all-gather.2.cloned.1.call-done = bf16[4,256,1536]{2,0,1:T(4,128)(2,1)} async-done(((bf16[4,256,384]{2,0,1:T(4,128)(2,1)}), bf16[4,256,1536]{2,0,1:T(4,128)(2,1)}) %all-gather.2.cloned.1.call-update) | async-done | bytes 3145744 | tf_op jit(solution)/shard_map/all_gather | solution.py:86
  112.8 2.5 %copy.72 = bf16[4,256,1536]{2,1,0:T(8,128)(2,1)S(1)} copy(bf16[4,256,1536]{2,0,1:T(4,128)(2,1)} %all-gather.2.cloned.1.call-done) | data formatting | bytes 6291456 | tf_op jit(solution)/shard_map/all_gather | solution.py:86
  115.3 1.8 convolution_convert_fusion.2
  117.0 1.8 convolution_convert_fusion.3
  118.8 2.1 reshape.235
  122.6 1.8 fusion.95
  124.5 3.0 %multiply_reduce_fusion = (f32[4,4,64]{2,0,1:T(4,128)S(1)}, bf16[4,4,64,320]{3,2,0,1:T(8,128)(2,1)S(1)}, f32[4,4,64,320]{3,2,0,1:T(8,128)}) fusion(f32[4,4,64,320]{3,2,0,1:T(8,128)} %get-tuple-element.40, f32[4,4,64]{2,0,1:T(4,128)S(1)} %get-tuple-element.39, bf16[4,64,4,64]{3,2,1,0:T(4,128)(2,1)S(1)} %reshape.219, ...), kind=kOutput, calls=%fused_computation.19 | convolution fusion | flops 44563456 | bytes 4071424 | tf_op jit(solution)/shard_map/wqhe,wkhe->whqk/dot_general | solution.py:150
  129.8 1.7 reshape.237
  131.8 3.1 %fusion.15 = bf16[4,320,4,64]{1,3,0,2:T(8,128)(2,1)S(1)} fusion(bf16[64,4,64,1]{0,2,3,1:T(8,128)(2,1)S(1)} %copy.101, f32[4,4,64,320]{3,2,0,1:T(8,128)} %get-tuple-element.41, f32[4,4,64]{2,0,1:T(4,128)S(1)} %get-tuple-element.27, f32[4,4,64,320]{3,2,0,1:T(8,128)} %get-tuple-element.40, f32[4,4,64]{2,0,1:T(4,128)S(1)} %get-tuple-element.39), kind=kOutput, calls=%fused_computation.24 | convolution fusion | flops 253296640 | bytes 3317760 | tf_op jit(solution)/shard_map/whqk,qhe->wkhe/dot_general | solution.py:157
  138.9 4.2 %convolution_bitcast_fusion = f32[1536,512]{1,0:T(8,128)S(1)} fusion(bf16[4,256,256]{2,1,0:T(8,128)(2,1)} %copy.116, bf16[4,256,256]{2,1,0:T(8,128)(2,1)} %copy.115, bf16[4,256,1536]{2,0,1:T(4,128)(2,1)} %all-gather.2.cloned.1.call-done), kind=kOutput, calls=%fused_computation.3 | convolution fusion | flops 1612709888 | bytes 7340032 | tf_op jit(solution)/shard_map/dot_general | solution.py:185
  143.1 3.3 %fusion.1 = f32[1536,512]{1,0:T(8,128)} fusion(f32[1536,512]{1,0:T(8,128)S(1)} %convolution_bitcast_fusion, f32[64,256]{0,1:T(8,128)S(1)} %get-tuple-element.42, f32[64,256]{0,1:T(8,128)S(1)} %get-tuple-element.43, bf16[64,1536]{1,0:T(8,128)(2,1)S(1)} %copy-done.1, f32[64]{0:T(128)S(1)} %add_rsqrt_fusion, f32[64]{0:T(128)S(1)} %broadcast_multiply_fusion.1), kind=kOutput, calls=%fused_computation.2 | convolution fusion | flops 605978624 | bytes 6619648 | tf_op jit(solution)/shard_map/dot_general | solution.py:188
  146.5 8.5 %reduce-scatter.7.cloned.1.call-done = bf16[384,256]{1,0:T(8,128)(2,1)} async-done(((bf16[1536,256]{1,0:T(8,128)(2,1)}), bf16[384,256]{1,0:T(8,128)(2,1)}) %reduce-scatter.7.cloned.1.call-update) | async-done | bytes 196624
  157.1 75.8 %reduce-scatter.5.cloned.1.call-done = f32[192,512]{1,0:T(8,128)} async-done(((f32[1536,512]{1,0:T(8,128)}), f32[192,512]{1,0:T(8,128)}) %reduce-scatter.5.cloned.1.call-update) | async-done | bytes 393232 | tf_op jit(solution)/shard_map/reduce_scatter | solution.py:195
  232.9 1.8 fusion.94
  (113 shorter events, 30.6 us)
Async XLA Ops:
  7.2 79.8 %copy-start = (bf16[256,1536]{1,0:T(8,128)(2,1)S(1)}, bf16[256,1536]{1,0:T(8,128)(2,1)}, u32[]{:S(2)}) copy-start(bf16[256,1536]{1,0:T(8,128)(2,1)} %param.18) | copy-start | bytes 2359300
  7.2 105.6 %all-gather.2.cloned.1.call-start = ((), (), s32[]{:S(2)}) async-start(), calls=%async_computation.2 | async-start | bytes 3932160 | tf_op jit(solution)/shard_map/all_gather | solution.py:86
  14.2 43.0 %collective-permute-start.1 = (bf16[256,384]{1,0:T(8,128)(2,1)S(1)}, bf16[256,384]{1,0:T(8,128)(2,1)S(1)}, u32[]{:S(2)}, u32[]{:S(2)}) collective-permute-start(bf16[256,384]{1,0:T(8,128)(2,1)S(1)} %bitcast.118), channel_id=1, source_target_pairs={{0,4},{4,8},{8,12},{12,16},{16,20},{20,24},{24,28},{1,5},{5,9},{9,... | collective-permute-start | bytes 589832 | tf_op jit(solution)/shard_map/ppermute | solution.py:13
  20.2 37.1 %collective-permute-start.3 = (bf16[256,384]{1,0:T(8,128)(2,1)S(1)}, bf16[256,384]{1,0:T(8,128)(2,1)S(1)}, u32[]{:S(2)}, u32[]{:S(2)}) collective-permute-start(bf16[256,384]{1,0:T(8,128)(2,1)S(1)} %bitcast.119), channel_id=1, source_target_pairs={{0,8},{4,12},{8,16},{12,20},{16,24},{20,28},{1,9},{5,13},{9,17},{1... | collective-permute-start | bytes 589832 | tf_op jit(solution)/shard_map/ppermute | solution.py:13
  24.8 32.5 %collective-permute-start.5 = (bf16[256,384]{1,0:T(8,128)(2,1)S(1)}, bf16[256,384]{1,0:T(8,128)(2,1)S(1)}, u32[]{:S(2)}, u32[]{:S(2)}) collective-permute-start(bf16[256,384]{1,0:T(8,128)(2,1)S(1)} %bitcast.120), channel_id=1, source_target_pairs={{0,12},{4,16},{8,20},{12,24},{16,28},{1,13},{5,17},{9,21},{13,25},... | collective-permute-start | bytes 589832 | tf_op jit(solution)/shard_map/ppermute | solution.py:13
  30.4 26.9 %collective-permute-start.7 = (bf16[256,384]{1,0:T(8,128)(2,1)S(1)}, bf16[256,384]{1,0:T(8,128)(2,1)S(1)}, u32[]{:S(2)}, u32[]{:S(2)}) collective-permute-start(bf16[256,384]{1,0:T(8,128)(2,1)S(1)} %bitcast.121), channel_id=1, source_target_pairs={{0,16},{4,20},{8,24},{12,28},{1,17},{5,21},{9,25},{13,29},{2,18},{... | collective-permute-start | bytes 589832 | tf_op jit(solution)/shard_map/ppermute | solution.py:13
  32.4 4.0 %collective-permute-start = (bf16[4]{0:T(256)(128)(2,1)S(1)}, bf16[4]{0:T(256)(128)(2,1)S(1)}, u32[]{:S(2)}, u32[]{:S(2)}) collective-permute-start(bf16[4]{0:T(256)(128)(2,1)S(1)} %get-tuple-element.5), channel_id=1, source_target_pairs={{0,4},{4,8},{8,12},{12,16},{16,20},{20,24},{24,28},{1,5},{5,9},{9,... | collective-permute-start | bytes 32 | tf_op jit(solution)/shard_map/ppermute | solution.py:13
  36.4 24.6 %copy-start.10 = (bf16[4]{0:T(256)(128)(2,1)}, bf16[4]{0:T(256)(128)(2,1)S(1)}, u32[]{:S(2)}) copy-start(bf16[4]{0:T(256)(128)(2,1)S(1)} %collective-permute-done) | copy-start | bytes 28
  36.4 15.7 %collective-permute-start.6 = (bf16[4]{0:T(256)(128)(2,1)S(1)}, bf16[4]{0:T(256)(128)(2,1)S(1)}, u32[]{:S(2)}, u32[]{:S(2)}) collective-permute-start(bf16[4]{0:T(256)(128)(2,1)S(1)} %get-tuple-element.14), channel_id=1, source_target_pairs={{0,16},{4,20},{8,24},{12,28},{1,17},{5,21},{9,25},{13,29},{2,18},{... | collective-permute-start | bytes 32 | tf_op jit(solution)/shard_map/ppermute | solution.py:13
  52.1 8.9 %copy-start.12 = (bf16[4]{0:T(256)(128)(2,1)}, bf16[4]{0:T(256)(128)(2,1)S(1)}, u32[]{:S(2)}) copy-start(bf16[4]{0:T(256)(128)(2,1)S(1)} %collective-permute-done.6) | copy-start | bytes 28
  52.1 2.6 %collective-permute-start.4 = (bf16[4]{0:T(256)(128)(2,1)S(1)}, bf16[4]{0:T(256)(128)(2,1)S(1)}, u32[]{:S(2)}, u32[]{:S(2)}) collective-permute-start(bf16[4]{0:T(256)(128)(2,1)S(1)} %get-tuple-element.16), channel_id=1, source_target_pairs={{0,12},{4,16},{8,20},{12,24},{16,28},{1,13},{5,17},{9,21},{13,25},... | collective-permute-start | bytes 32 | tf_op jit(solution)/shard_map/ppermute | solution.py:13
  54.7 6.4 %copy-start.14 = (bf16[4]{0:T(256)(128)(2,1)}, bf16[4]{0:T(256)(128)(2,1)S(1)}, u32[]{:S(2)}) copy-start(bf16[4]{0:T(256)(128)(2,1)S(1)} %collective-permute-done.4) | copy-start | bytes 28
  54.7 2.6 %collective-permute-start.2 = (bf16[4]{0:T(256)(128)(2,1)S(1)}, bf16[4]{0:T(256)(128)(2,1)S(1)}, u32[]{:S(2)}, u32[]{:S(2)}) collective-permute-start(bf16[4]{0:T(256)(128)(2,1)S(1)} %get-tuple-element.18), channel_id=1, source_target_pairs={{0,8},{4,12},{8,16},{12,20},{16,24},{20,28},{1,9},{5,13},{9,17},{1... | collective-permute-start | bytes 32 | tf_op jit(solution)/shard_map/ppermute | solution.py:13
  57.2 3.8 %copy-start.16 = (bf16[4]{0:T(256)(128)(2,1)}, bf16[4]{0:T(256)(128)(2,1)S(1)}, u32[]{:S(2)}) copy-start(bf16[4]{0:T(256)(128)(2,1)S(1)} %collective-permute-done.2) | copy-start | bytes 28
  74.0 1.9 copy-start.5
  75.5 1.8 copy-start.8
  75.5 79.4 %reduce-scatter.7.cloned.1.call-start = ((), (), s32[]{:S(2)}) async-start(), calls=%async_computation.4 | async-start | bytes 983040
  76.0 10.9 %copy-start.11 = (bf16[4]{0:T(256)(128)(2,1)S(1)}, bf16[4]{0:T(256)(128)(2,1)}, u32[]{:S(2)}) copy-start(bf16[4]{0:T(256)(128)(2,1)} %copy-done.10) | copy-start | bytes 28
  76.0 10.8 %copy-start.13 = (bf16[4]{0:T(256)(128)(2,1)S(1)}, bf16[4]{0:T(256)(128)(2,1)}, u32[]{:S(2)}) copy-start(bf16[4]{0:T(256)(128)(2,1)} %copy-done.12) | copy-start | bytes 28
  76.0 10.8 %copy-start.15 = (bf16[4]{0:T(256)(128)(2,1)S(1)}, bf16[4]{0:T(256)(128)(2,1)}, u32[]{:S(2)}) copy-start(bf16[4]{0:T(256)(128)(2,1)} %copy-done.14) | copy-start | bytes 28
  76.0 10.8 %copy-start.17 = (bf16[4]{0:T(256)(128)(2,1)S(1)}, bf16[4]{0:T(256)(128)(2,1)}, u32[]{:S(2)}) copy-start(bf16[4]{0:T(256)(128)(2,1)} %copy-done.16) | copy-start | bytes 28
  87.6 36.9 %copy-start.2 = (bf16[4,64,4,64]{3,2,1,0:T(4,128)(2,1)}, bf16[4,64,4,64]{3,2,1,0:T(4,128)(2,1)S(1)}, u32[]{:S(2)}) copy-start(bf16[4,64,4,64]{3,2,1,0:T(4,128)(2,1)S(1)} %reshape.219) | copy-start | bytes 393220
  118.8 2.6 %copy-start.7 = (bf16[1024,256]{1,0:T(8,128)(2,1)S(1)}, bf16[1024,256]{1,0:T(8,128)(2,1)}, u32[]{:S(2)}) copy-start(bf16[1024,256]{1,0:T(8,128)(2,1)} %convolution_convert_fusion.2) | copy-start | bytes 1572868
  131.5 101.4 %reduce-scatter.5.cloned.1.call-start = ((), (), s32[]{:S(2)}) async-start(), calls=%async_computation.3 | async-start | bytes 3538944 | tf_op jit(solution)/shard_map/reduce_scatter | solution.py:195
  (5 other events, 6.3 us)
Sparse Core Ops, SparseCore 0:
  75.6 37.1 all-gather.1
  131.6 23.2 reduce-scatter.6
  158.5 74.3 reduce-scatter.4
where the time goes:
time: 242 us; the launch traced here: 241 us
  waiting for transfers between devices  115 us (48%)
  starting transfers between devices  34.8 us (14%)
  matrix products  31.2 us (13%)
  blocking collectives  22.4 us (9%)
  local copies, waits for them, and re-layouts  15.8 us (7%)
  between operations  14.3 us (6%)
  other arithmetic  7.98 us (3%)
    reduce_scatter x1, waiting for transfers between devices, local(): lax.psum_scatter((media_part + latent_term) * inverse_slots, 'dp', scatte...  75.8 us
    ppermute x8, starting transfers between devices, from_behind(): return lax.ppermute(block, axis, route)  34.5 us
    all_gather x1, waiting for transfers between devices, local(): lax.all_gather(normed_part, 'mp', axis=2, tiled=True)  25.2 us
    psum x1, blocking collectives, local(): first_all, square_all = lax.psum((first_sum, square_sum), 'mp')  12.9 us
    all_gather x1, blocking collectives, local(): lax.all_gather(cotangent, 'mp', axis=2, tiled=True)  9.53 us
    unnamed x4, waiting for transfers between devices  8.5 us
    unnamed x42, local copies, waits for them, and re-layouts  6.93 us
    ppermute x8, waiting for transfers between devices, from_behind(): return lax.ppermute(block, axis, route)  5.09 us
  transfers between devices with their start and end apart: 11, of which 7 were waited for; matrix products, arithmetic and copies ran while one was open for 9% of the time, Pallas kernels for 0%

commit v1 on v0

--- a/solution.py
+++ b/solution.py
@@ -5,6 +5,12 @@
 
 HEAD = 64
 norm_epsilon = 1e-05
+
+
+def link_set_over_axis(w_in):
+    return jnp.concatenate(
+        lax.all_to_all(jnp.stack([w_in for _ in range(lax.axis_size("mp"))], axis=0), "mp", 0, 0), 2
+    )
 
 
 def from_behind(block, axis, distance):
@@ -83,7 +89,7 @@
     spread = square_all / model_width - average * average
     normed_part = ((values32 - average) * lax.rsqrt(spread + norm_epsilon)).astype(jnp.bfloat16)
     normed, cot_full = (
-        lax.all_gather(normed_part, "mp", axis=2, tiled=True),
+        link_set_over_axis(normed_part),
         lax.all_gather(cotangent, "mp", axis=2, tiled=True),
     )
     normed_flat = normed.reshape(work_slots * image_tokens, model_width)

time: 242 us -> 261 us (1.079)
  blocking collectives: 22.4 us -> 53.4 us
  waiting for transfers between devices: 115 us -> 95.5 us
  starting transfers between devices: 34.8 us -> 39.5 us
  local copies, waits for them, and re-layouts: 15.8 us -> 20 us
    all_gather x1, blocking collectives: 9.53 us -> 40.5 us  [local(): lax.all_gather(cotangent, 'mp', axis=2, tiled=True)]
    all_gather x1 -> x0, waiting for transfers between devices: 25.2 us -> none  [local(): lax.all_gather(normed_part, 'mp', axis=2, tiled=True)]
    unnamed x4 -> x3, waiting for transfers between devices: 8.5 us -> 14.6 us
    all_to_all x0 -> x1, starting transfers between devices: none -> 4.77 us  [link_set_over_axis(): lax.all_to_all(jnp.stack([w_in for _ in range(lax.axis_size('mp'))], axis...]
    reshape x0 -> x1, local copies, waits for them, and re-layouts: none -> 4.41 us  [link_set_over_axis(): jnp.concatenate(lax.all_to_all(jnp.stack([w_in for _ in range(lax.axis_si...]
    unnamed x42 -> x31, local copies, waits for them, and re-layouts: 6.93 us -> 7.25 us
  transfers between devices with their start and end apart: 11 -> 11, of which waited for: 7 -> 6; matrix products, arithmetic and copies ran while one was open for 9% -> 8% of each run, Pallas kernels for 0% -> 0%
where the time goes in v1:
time: 261 us; the launch traced here: 260 us
  waiting for transfers between devices  95.5 us (37%)
  blocking collectives  53.4 us (20%)
  starting transfers between devices  39.5 us (15%)
  matrix products  29 us (11%)
  local copies, waits for them, and re-layouts  20 us (8%)
  between operations  14.7 us (6%)
  other arithmetic  8.29 us (3%)
    reduce_scatter x1, waiting for transfers between devices, local(): lax.psum_scatter((media_part + latent_term) * inverse_slots, 'dp', scatte...  76 us
    all_gather x1, blocking collectives, local(): lax.all_gather(cotangent, 'mp', axis=2, tiled=True)  40.5 us
    ppermute x8, starting transfers between devices, from_behind(): return lax.ppermute(block, axis, route)  34.5 us
    unnamed x3, waiting for transfers between devices  14.6 us
    psum x1, blocking collectives, local(): first_all, square_all = lax.psum((first_sum, square_sum), 'mp')  12.9 us
    unnamed x31, local copies, waits for them, and re-layouts  7.25 us
  transfers between devices with their start and end apart: 11, of which 6 were waited for; matrix products, arithmetic and copies ran while one was open for 8% of the time, Pallas kernels for 0%

profile of v1, /device:TPU:0, one launch (start us, length us, event | category | flops | bytes accessed | tf_op | source)
XLA Modules:
  0.0 260.4 jit_solution(2062857427746339927)
XLA Ops:
  11.1 1.7 add_convert_fusion
  14.2 4.9 %collective-permute-start.1 = (bf16[256,384]{1,0:T(8,128)(2,1)S(1)}, bf16[256,384]{1,0:T(8,128)(2,1)S(1)}, u32[]{:S(2)}, u32[]{:S(2)}) collective-permute-start(bf16[256,384]{1,0:T(8,128)(2,1)S(1)} %bitcast.125), channel_id=1, source_target_pairs={{0,4},{4,8},{8,12},{12,16},{16,20},{20,24},{24,28},{1,5},{5,9},{9,... | collective-permute-start | bytes 589832 | tf_op jit(solution)/shard_map/ppermute | solution.py:19
  20.2 3.5 %collective-permute-start.3 = (bf16[256,384]{1,0:T(8,128)(2,1)S(1)}, bf16[256,384]{1,0:T(8,128)(2,1)S(1)}, u32[]{:S(2)}, u32[]{:S(2)}) collective-permute-start(bf16[256,384]{1,0:T(8,128)(2,1)S(1)} %bitcast.126), channel_id=1, source_target_pairs={{0,8},{4,12},{8,16},{12,20},{16,24},{20,28},{1,9},{5,13},{9,17},{1... | collective-permute-start | bytes 589832 | tf_op jit(solution)/shard_map/ppermute | solution.py:19
  24.8 4.6 %collective-permute-start.5 = (bf16[256,384]{1,0:T(8,128)(2,1)S(1)}, bf16[256,384]{1,0:T(8,128)(2,1)S(1)}, u32[]{:S(2)}, u32[]{:S(2)}) collective-permute-start(bf16[256,384]{1,0:T(8,128)(2,1)S(1)} %bitcast.127), channel_id=1, source_target_pairs={{0,12},{4,16},{8,20},{12,24},{16,28},{1,13},{5,17},{9,21},{13,25},... | collective-permute-start | bytes 589832 | tf_op jit(solution)/shard_map/ppermute | solution.py:19
  30.5 1.9 collective-permute-start.7
  32.5 2.7 %collective-permute-start = (bf16[4]{0:T(256)(128)(2,1)S(1)}, bf16[4]{0:T(256)(128)(2,1)S(1)}, u32[]{:S(2)}, u32[]{:S(2)}) collective-permute-start(bf16[4]{0:T(256)(128)(2,1)S(1)} %get-tuple-element.5), channel_id=1, source_target_pairs={{0,4},{4,8},{8,12},{12,16},{16,20},{20,24},{24,28},{1,5},{5,9},{9,... | collective-permute-start | bytes 32 | tf_op jit(solution)/shard_map/ppermute | solution.py:19
  36.5 14.3 %collective-permute-start.6 = (bf16[4]{0:T(256)(128)(2,1)S(1)}, bf16[4]{0:T(256)(128)(2,1)S(1)}, u32[]{:S(2)}, u32[]{:S(2)}) collective-permute-start(bf16[4]{0:T(256)(128)(2,1)S(1)} %get-tuple-element.14), channel_id=1, source_target_pairs={{0,16},{4,20},{8,24},{12,28},{1,17},{5,21},{9,25},{13,29},{2,18},{... | collective-permute-start | bytes 32 | tf_op jit(solution)/shard_map/ppermute | solution.py:19
  57.4 3.6 %convert_reduce_fusion = (f32[4,256]{0,1:T(8,128)S(1)}, f32[4,256]{0,1:T(8,128)S(1)}, bf16[4,256,384]{2,0,1:T(4,128)(2,1)S(1)}) fusion(f32[256,384]{1,0:T(8,128)S(1)} %convert_element_type.173, f32[4]{0:T(128)S(1)} %convert_element_type.171, f32[256,384]{1,0:T(8,128)S(1)} %convert_element_type.169, f32[4]{0:T(128)S(1)} %convert_element_type.167, ...), kind=kOutput, calls=%fused_computation.7 | convolution fusion | flops 11401248 | bytes 3940456 | tf_op jit(solution)/shard_map/sw,std->wtd/dot_general | solution.py:67
  61.0 12.9 %all-reduce = (f32[4,256,1]{0,1,2:T(8,128)S(1)}, f32[4,256,1]{0,1,2:T(8,128)S(1)}) all-reduce(f32[4,256,1]{0,1,2:T(8,128)S(1)} %bitcast.130, f32[4,256,1]{0,1,2:T(8,128)S(1)} %bitcast.129), channel_id=1, replica_groups=mesh['dp'=8,'mp'=4] {'mp'}, use_global_device_ids=true, to_apply=%region_13.14 | all-reduce | flops 2048 | bytes 16384 | tf_op jit(solution)/shard_map/psum | solution.py:87
  74.8 2.1 stack.2
  76.9 4.8 %all-to-all-start = ((bf16[4,4,256,384]{3,2,1,0:T(8,128)(2,1)}), bf16[4,4,256,384]{3,2,1,0:T(8,128)(2,1)}, u32[]{:S(2)}, u32[]{:S(2)}) async-start(bf16[4,4,256,384]{3,2,1,0:T(8,128)(2,1)} %stack.2), calls=%async_computation | async-start | bytes 6291456 | tf_op jit(solution)/shard_map/all_to_all | solution.py:12
  83.1 40.5 %all_gather.3 = bf16[4,64,1536]{2,1,0:T(8,128)(2,1)S(1)} all-gather(bf16[4,64,384]{2,1,0:T(8,128)(2,1)S(1)} %copy-done.11), channel_id=1, replica_groups=mesh['dp'=8,'mp'=4] {'mp'}, dimensions={2}, use_global_device_ids=true | all-gather | bytes 983040 | tf_op jit(solution)/shard_map/all_gather | solution.py:93
  124.4 4.4 %copy.69 = bf16[4,256,4,384]{3,2,1,0:T(4,128)(2,1)S(1)} copy(bf16[4,256,4,384]{3,1,0,2:T(8,128)(2,1)} %bitcast.16) | data formatting | bytes 6291456 | tf_op jit(solution)/shard_map/reshape | solution.py:11
  131.0 1.8 convolution_convert_fusion.3
  134.8 1.8 fusion.90
  136.7 3.0 %multiply_reduce_fusion = (f32[4,4,64]{2,0,1:T(4,128)S(1)}, bf16[4,4,64,320]{3,2,0,1:T(8,128)(2,1)S(1)}, f32[4,4,64,320]{3,2,0,1:T(8,128)}) fusion(f32[4,4,64,320]{3,2,0,1:T(8,128)} %get-tuple-element.40, f32[4,4,64]{2,0,1:T(4,128)S(1)} %get-tuple-element.39, bf16[4,64,4,64]{3,2,1,0:T(4,128)(2,1)S(1)} %reshape.223, ...), kind=kOutput, calls=%fused_computation.18 | convolution fusion | flops 44563456 | bytes 4071424 | tf_op jit(solution)/shard_map/wqhe,wkhe->whqk/dot_general | solution.py:156
  142.0 1.7 reshape.241
  144.0 3.1 %fusion.15 = bf16[4,320,4,64]{1,3,0,2:T(8,128)(2,1)S(1)} fusion(bf16[64,4,64,1]{0,2,3,1:T(8,128)(2,1)S(1)} %copy.96, f32[4,4,64,320]{3,2,0,1:T(8,128)} %get-tuple-element.41, f32[4,4,64]{2,0,1:T(4,128)S(1)} %get-tuple-element.27, f32[4,4,64,320]{3,2,0,1:T(8,128)} %get-tuple-element.40, f32[4,4,64]{2,0,1:T(4,128)S(1)} %get-tuple-element.39), kind=kOutput, calls=%fused_computation.23 | convolution fusion | flops 253296640 | bytes 3317760 | tf_op jit(solution)/shard_map/whqk,qhe->wkhe/dot_general | solution.py:163
  149.2 1.3 copy.86
  151.7 4.0 %fusion.93 = f32[1536,512]{1,0:T(8,128)S(1)} fusion(bf16[1024,1536]{1,0:T(8,128)(2,1)} %bitcast.115, bf16[1024,512]{1,0:T(8,128)(2,1)} %bitcast.120), kind=kOutput, calls=%fused_computation.129 | convolution fusion | flops 1610612736 | bytes 7340032 | tf_op jit(solution)/shard_map/dot_general | solution.py:191
  155.7 3.3 %fusion.1 = f32[1536,512]{1,0:T(8,128)} fusion(f32[1536,512]{1,0:T(8,128)S(1)} %fusion.93, f32[64,256]{0,1:T(8,128)S(1)} %get-tuple-element.42, f32[64,256]{0,1:T(8,128)S(1)} %get-tuple-element.43, bf16[64,1536]{1,0:T(8,128)(2,1)S(1)} %copy-done.1, f32[64]{0:T(128)S(1)} %add_rsqrt_fusion, f32[64]{0:T(128)S(1)} %broadcast_multiply_fusion.1), kind=kOutput, calls=%fused_computation.2 | convolution fusion | flops 605978624 | bytes 6619648 | tf_op jit(solution)/shard_map/dot_general | solution.py:194
  159.1 14.5 %reduce-scatter.7.cloned.1.call-done = bf16[384,256]{1,0:T(8,128)(2,1)} async-done(((bf16[1536,256]{1,0:T(8,128)(2,1)}), bf16[384,256]{1,0:T(8,128)(2,1)}) %reduce-scatter.7.cloned.1.call-update) | async-done | bytes 196624
  175.8 76.0 %reduce-scatter.5.cloned.1.call-done = f32[192,512]{1,0:T(8,128)} async-done(((f32[1536,512]{1,0:T(8,128)}), f32[192,512]{1,0:T(8,128)}) %reduce-scatter.5.cloned.1.call-update) | async-done | bytes 393232 | tf_op jit(solution)/shard_map/reduce_scatter | solution.py:201
  251.8 1.8 fusion.89
  (105 shorter events, 31.4 us)
Async XLA Ops:
  7.2 116.6 %copy-start = (bf16[256,1536]{1,0:T(8,128)(2,1)S(1)}, bf16[256,1536]{1,0:T(8,128)(2,1)}, u32[]{:S(2)}) copy-start(bf16[256,1536]{1,0:T(8,128)(2,1)} %param.18) | copy-start | bytes 2359300
  14.2 43.0 %collective-permute-start.1 = (bf16[256,384]{1,0:T(8,128)(2,1)S(1)}, bf16[256,384]{1,0:T(8,128)(2,1)S(1)}, u32[]{:S(2)}, u32[]{:S(2)}) collective-permute-start(bf16[256,384]{1,0:T(8,128)(2,1)S(1)} %bitcast.125), channel_id=1, source_target_pairs={{0,4},{4,8},{8,12},{12,16},{16,20},{20,24},{24,28},{1,5},{5,9},{9,... | collective-permute-start | bytes 589832 | tf_op jit(solution)/shard_map/ppermute | solution.py:19
  20.2 37.0 %collective-permute-start.3 = (bf16[256,384]{1,0:T(8,128)(2,1)S(1)}, bf16[256,384]{1,0:T(8,128)(2,1)S(1)}, u32[]{:S(2)}, u32[]{:S(2)}) collective-permute-start(bf16[256,384]{1,0:T(8,128)(2,1)S(1)} %bitcast.126), channel_id=1, source_target_pairs={{0,8},{4,12},{8,16},{12,20},{16,24},{20,28},{1,9},{5,13},{9,17},{1... | collective-permute-start | bytes 589832 | tf_op jit(solution)/shard_map/ppermute | solution.py:19
  24.8 10.5 %copy-start.1 = (bf16[64,1536]{1,0:T(8,128)(2,1)S(1)}, bf16[64,1536]{1,0:T(8,128)(2,1)}, u32[]{:S(2)}) copy-start(bf16[64,1536]{1,0:T(8,128)(2,1)} %param.14) | copy-start | bytes 589828
  24.8 32.5 %collective-permute-start.5 = (bf16[256,384]{1,0:T(8,128)(2,1)S(1)}, bf16[256,384]{1,0:T(8,128)(2,1)S(1)}, u32[]{:S(2)}, u32[]{:S(2)}) collective-permute-start(bf16[256,384]{1,0:T(8,128)(2,1)S(1)} %bitcast.127), channel_id=1, source_target_pairs={{0,12},{4,16},{8,20},{12,24},{16,28},{1,13},{5,17},{9,21},{13,25},... | collective-permute-start | bytes 589832 | tf_op jit(solution)/shard_map/ppermute | solution.py:19
  30.5 26.8 %collective-permute-start.7 = (bf16[256,384]{1,0:T(8,128)(2,1)S(1)}, bf16[256,384]{1,0:T(8,128)(2,1)S(1)}, u32[]{:S(2)}, u32[]{:S(2)}) collective-permute-start(bf16[256,384]{1,0:T(8,128)(2,1)S(1)} %bitcast.128), channel_id=1, source_target_pairs={{0,16},{4,20},{8,24},{12,28},{1,17},{5,21},{9,25},{13,29},{2,18},{... | collective-permute-start | bytes 589832 | tf_op jit(solution)/shard_map/ppermute | solution.py:19
  32.5 4.0 %collective-permute-start = (bf16[4]{0:T(256)(128)(2,1)S(1)}, bf16[4]{0:T(256)(128)(2,1)S(1)}, u32[]{:S(2)}, u32[]{:S(2)}) collective-permute-start(bf16[4]{0:T(256)(128)(2,1)S(1)} %get-tuple-element.5), channel_id=1, source_target_pairs={{0,4},{4,8},{8,12},{12,16},{16,20},{20,24},{24,28},{1,5},{5,9},{9,... | collective-permute-start | bytes 32 | tf_op jit(solution)/shard_map/ppermute | solution.py:19
  36.5 15.5 %collective-permute-start.6 = (bf16[4]{0:T(256)(128)(2,1)S(1)}, bf16[4]{0:T(256)(128)(2,1)S(1)}, u32[]{:S(2)}, u32[]{:S(2)}) collective-permute-start(bf16[4]{0:T(256)(128)(2,1)S(1)} %get-tuple-element.14), channel_id=1, source_target_pairs={{0,16},{4,20},{8,24},{12,28},{1,17},{5,21},{9,25},{13,29},{2,18},{... | collective-permute-start | bytes 32 | tf_op jit(solution)/shard_map/ppermute | solution.py:19
  52.1 2.6 collective-permute-start.4
  54.6 2.6 collective-permute-start.2
  76.9 5.1 %copy-start.8 = (bf16[1536,256]{1,0:T(8,128)(2,1)S(1)}, bf16[1536,256]{1,0:T(8,128)(2,1)}, u32[]{:S(2)}) copy-start(bf16[1536,256]{1,0:T(8,128)(2,1)} %param.16) | copy-start | bytes 2359300
  76.9 5.5 %copy-start.9 = (bf16[1536,256]{1,0:T(8,128)(2,1)S(1)}, bf16[1536,256]{1,0:T(8,128)(2,1)}, u32[]{:S(2)}) copy-start(bf16[1536,256]{1,0:T(8,128)(2,1)} %param.17) | copy-start | bytes 2359300
  76.9 47.5 %all-to-all-start = ((bf16[4,4,256,384]{3,2,1,0:T(8,128)(2,1)}), bf16[4,4,256,384]{3,2,1,0:T(8,128)(2,1)}, u32[]{:S(2)}, u32[]{:S(2)}) async-start(bf16[4,4,256,384]{3,2,1,0:T(8,128)(2,1)} %stack.2), calls=%async_computation | async-start | bytes 6291456 | tf_op jit(solution)/shard_map/all_to_all | solution.py:12
  81.7 1.2 copy-start.12
  81.7 1.4 copy-start.11
  81.7 91.9 %reduce-scatter.7.cloned.1.call-start = ((), (), s32[]{:S(2)}) async-start(), calls=%async_computation.4 | async-start | bytes 983040
  124.3 12.4 %copy-start.4 = (bf16[4,64,4,64]{3,2,1,0:T(4,128)(2,1)}, bf16[4,64,4,64]{3,2,1,0:T(4,128)(2,1)S(1)}, u32[]{:S(2)}) copy-start(bf16[4,64,4,64]{3,2,1,0:T(4,128)(2,1)S(1)} %reshape.223) | copy-start | bytes 393220
  129.3 1.7 copy-start.2
  132.8 1.1 copy-start.10
  139.7 0.9 copy-start.6
  143.8 108.0 %reduce-scatter.5.cloned.1.call-start = ((), (), s32[]{:S(2)}) async-start(), calls=%async_computation.3 | async-start | bytes 3538944 | tf_op jit(solution)/shard_map/reduce_scatter | solution.py:201
  147.2 1.0 copy-start.5
  147.2 1.5 copy-start.7
  147.3 0.9 copy-start.3
Sparse Core Ops, SparseCore 0:
  143.9 29.6 reduce-scatter.6
  177.2 74.5 reduce-scatter.4
